TPU v7x, 32 devices: a whole 2x2x4 slice. The times are simulated.
32 devices in a mesh: doc: 8 (over z, y), seq: 4 (over x, core).
Axes of the slice: x: 2, y: 2, z: 4, core: 2. Of those that a mesh axis runs over, the one named last changes fastest.
Arguments:
- queries: bfloat16 [16384, 512], P(('doc', 'seq')), parts along dimension 0, may hold values from -5 to 5
- teacher_keys: bfloat16 [16384, 128], P(('doc', 'seq')), parts along dimension 0, may hold values from -5 to 5
- teacher_values: bfloat16 [16384, 128], P(('doc', 'seq')), parts along dimension 0, may hold values from -5 to 5
- beacon_starts: int32 [1024], P(('doc', 'seq')), parts along dimension 0, may hold values from 0 to 511, as said below
Outputs:
- output_gap: bfloat16 [16384, 512], P(('doc', 'seq')), parts along dimension 0
- beacon_key_grad: float32 [1024, 128], P(('doc', 'seq')), parts along dimension 0
- beacon_value_grad: float32 [1024, 128], P(('doc', 'seq')), parts along dimension 0
There are 8 independent parts, one for each index of `doc`. A program takes and returns all parts, laid end to end along the dimension named above; each array names one. Nothing has to cross between parts.
Inputs may be any that keep to these rules, and one draw needn't show every extreme that they name: `beacon_starts`: each aligned block of 32 entries belongs to one shard of 512 tokens: its first entry is 0 and its entries rise strictly.
All inputs are finite; a program needn't handle non-finite values.
Results may differ from a plain program's by a relative error of at most 0.009.
Values may be sent and summed in bfloat16 or wider, within the bound.
A program may use at most 192 MiB of HBM per device.

v0:
```python
import jax
import jax.numpy as jnp
from jax import lax
from jax.sharding import PartitionSpec as P


def fresh_state(row_count, head_size):
    return (
        jnp.full((row_count,), -1e30, jnp.float32),
        jnp.zeros((row_count,), jnp.float32),
        jnp.zeros((row_count, head_size), jnp.float32),
    )


def attend_block(state, query_rows, query_pos, piece, head_size, scaling):
    running, total_weight, accum = state
    key_pos = jnp.arange(piece.shape[0], dtype=jnp.int32)
    scores = (
        jnp.dot(query_rows, piece[:, :head_size].T, preferred_element_type=jnp.float32) * scaling
    )
    scores = jnp.where(key_pos[None, :] <= query_pos[:, None], scores, -jnp.inf)
    highest = jnp.maximum(running, jnp.max(scores, axis=1))
    weights = jnp.exp(scores - highest[:, None])
    total_weight = jnp.sum(weights, axis=1)
    accum = jnp.dot(
        weights.astype(jnp.bfloat16), piece[:, head_size:], preferred_element_type=jnp.float32
    )
    return (highest, total_weight, accum)


def body(queries, teacher_keys, teacher_values, beacon_starts):
    tok_here, head_size = teacher_keys.shape
    heads = queries.shape[1] // head_size
    seq_index = lax.axis_index("seq")
    scaling = head_size ** (-0.5)
    beac_here = beacon_starts.shape[0]
    joined = jnp.concatenate([teacher_keys, teacher_values], axis=1)
    positions = jnp.arange(tok_here, dtype=jnp.int32)
    endings = jnp.concatenate([beacon_starts[1:], jnp.full((1,), tok_here, jnp.int32)])
    member = (positions[None, :] >= beacon_starts[:, None]) & (
        positions[None, :] < endings[:, None]
    )
    counts = jnp.sum(member.astype(jnp.float32), axis=1)
    pooled = jnp.dot(member.astype(jnp.bfloat16), joined, preferred_element_type=jnp.float32)
    beacon_rows = (pooled / counts[:, None]).astype(jnp.bfloat16)
    beacons = lax.all_gather(beacon_rows, "seq", axis=0, tiled=True)
    first_token = seq_index * tok_here
    row_count = tok_here * heads
    query_rows = queries.reshape(row_count, head_size)
    local_pos = jnp.arange(row_count, dtype=jnp.int32) // heads
    initial = fresh_state(row_count, head_size)
    folded = attend_block(
        initial,
        query_rows,
        first_token + local_pos,
        lax.all_gather(joined, "seq", axis=0, tiled=True),
        head_size,
        scaling,
    )
    teacher = folded[2] / folded[1][:, None]
    beacon_count = beacons.shape[0]
    owners = jnp.arange(beacon_count, dtype=jnp.int32) // beac_here
    keys_all = jnp.concatenate([beacons[:, :head_size], teacher_keys], axis=0)
    values_all = jnp.concatenate([beacons[:, head_size:], teacher_values], axis=0)
    visible = jnp.concatenate(
        [
            jnp.broadcast_to(owners[None, :] < seq_index, (row_count, beacon_count)),
            positions[None, :] <= local_pos[:, None],
        ],
        axis=1,
    )
    student_scores = jnp.where(
        visible,
        jnp.dot(query_rows, keys_all.T, preferred_element_type=jnp.float32) * scaling,
        -jnp.inf,
    )
    student_weights = jnp.exp(student_scores - jnp.max(student_scores, axis=1, keepdims=True))
    student_probs = student_weights / jnp.sum(student_weights, axis=1, keepdims=True)
    probs_low = student_probs.astype(jnp.bfloat16)
    student = jnp.dot(probs_low, values_all, preferred_element_type=jnp.float32)
    output_gap = (student - teacher).astype(jnp.bfloat16)
    prob_grad = jnp.dot(output_gap, values_all.T, preferred_element_type=jnp.float32)
    row_dot = jnp.sum(student_probs * prob_grad, axis=1, keepdims=True)
    score_grad = (student_probs * (prob_grad - row_dot)).astype(jnp.bfloat16)
    grad_keys = (
        jnp.dot(score_grad[:, :beacon_count].T, query_rows, preferred_element_type=jnp.float32)
        * scaling
    )
    grad_values = jnp.dot(
        probs_low[:, :beacon_count].T, output_gap, preferred_element_type=jnp.float32
    )
    grads = lax.psum_scatter(
        jnp.concatenate([grad_keys, grad_values], axis=1).astype(jnp.bfloat16),
        "seq",
        scatter_dimension=0,
        tiled=True,
    ).astype(jnp.float32)
    return (
        output_gap.reshape(tok_here, heads * head_size),
        grads[:, :head_size],
        grads[:, head_size:],
    )


def solution(mesh):
    in_specs = (
        P(("doc", "seq"), None),
        P(("doc", "seq"), None),
        P(("doc", "seq"), None),
        P(("doc", "seq")),
    )
    out_specs = (P(("doc", "seq"), None), P(("doc", "seq"), None), P(("doc", "seq"), None))
    return jax.shard_map(body, mesh=mesh, in_specs=in_specs, out_specs=out_specs, check_vma=False)
```

profile of v0, /device:TPU:0, one launch (start us, length us, event | category | flops | bytes accessed | tf_op | source)
XLA Modules:
  0.0 75.1 jit_solution(14301747394029188037)
XLA Ops:
  7.2 0.0 all-gather.2.cloned.1.call-start
  7.2 0.9 %constant_dynamic-update-slice_fusion.1 = bf16[512,256]{1,0:T(8,128)(2,1)S(1)} fusion(bf16[512,128]{1,0:T(8,128)(2,1)} %param.5), kind=kLoop, calls=%fused_computation.49 | loop fusion | bytes 262144
  8.1 0.9 %constant_dynamic-update-slice_fusion = bf16[512,256]{1,0:T(8,128)(2,1)S(1)} fusion(bf16[512,256]{1,0:T(8,128)(2,1)S(1)} %constant_dynamic-update-slice_fusion.1, bf16[512,128]{1,0:T(8,128)(2,1)} %param.6), kind=kLoop, calls=%fused_computation.48 | loop fusion | bytes 262144 | tf_op jit(solution)/shard_map/concatenate | solution.py:37
  9.1 0.7 copy-done.3
  9.8 0.0 all-gather.2.cloned.1.call-update
  9.8 0.0 reduce-scatter.4.cloned.1.call-start
  9.9 0.7 slice.27
  10.6 0.1 pad_add_fusion
  10.7 0.8 %convert_reduce_fusion = f32[32]{0:T(128)S(1)} fusion(s32[32]{0:T(128)S(1)} %pad_add_fusion, s32[32]{0:T(128)} %param.7), kind=kLoop, calls=%fused_computation.35 | loop fusion | flops 81888 | bytes 384 | tf_op jit(solution)/shard_map/reduce_sum | solution.py:43
  11.6 1.2 %fusion.12 = bf16[32,256]{1,0:T(8,128)(2,1)S(1)} fusion(bf16[512,256]{1,0:T(8,128)(2,1)} %copy-done.3, s32[32]{0:T(128)S(1)} %pad_add_fusion, s32[32]{0:T(128)} %param.7, f32[32]{0:T(128)S(1)} %convert_reduce_fusion), kind=kOutput, calls=%fused_computation.20 | convolution fusion | flops 8454144 | bytes 278912 | tf_op jit(solution)/shard_map/dot_general | solution.py:44
  12.7 6.2 %all_gather.6 = bf16[128,256]{1,0:T(8,128)(2,1)S(1)} all-gather(bf16[32,256]{1,0:T(8,128)(2,1)S(1)} %fusion.12), channel_id=1, replica_groups=mesh['doc'=8,'seq'=4] {'seq'}, dimensions={0}, use_global_device_ids=true | all-gather | bytes 81920 | tf_op jit(solution)/shard_map/all_gather | solution.py:46
  18.9 0.6 iota_compare_fusion.1
  19.6 1.4 %reshape.53 = bf16[2048,128]{1,0:T(8,128)(2,1)S(1)} reshape(bf16[512,512]{1,0:T(8,128)(2,1)} %param.4) | data formatting | bytes 1048576 | tf_op jit(solution)/shard_map/reshape | solution.py:49
  21.0 2.2 %fusion.41 = (f32[2048]{0:T(1024)S(1)}, f32[2048,640]{0,1:T(8,128)S(1)}) fusion(bf16[2048,128]{1,0:T(8,128)(2,1)S(1)} %reshape.53, bf16[512,128]{1,0:T(8,128)(2,1)} %param.5, bf16[128,128]{1,0:T(8,128)(2,1)S(1)} %get-tuple-element.17, pred[2048,512]{0,1:T(32,128)(4,1)S(1)} %iota_compare_fusion.1, pred[640]{0:T(1024)(128)(4,1)S(1)} %pad.8.clone), kind=kOutput, calls=%fused_computation.66 | convolution fusion | flops 341112832 | bytes 6988416 | tf_op jit(solution)/shard_map/dot_general | solution.py:74
  23.3 0.7 fusion.6
  24.0 3.2 %fusion.37 = (bf16[2048,640]{0,1:T(8,128)(2,1)S(1)}, f32[2048,640]{0,1:T(8,128)}) fusion(f32[2048]{0:T(1024)S(1)} %fusion.6, f32[2048,640]{0,1:T(8,128)S(1)} %get-tuple-element.21, f32[2048]{0:T(1024)S(1)} %get-tuple-element.20), kind=kLoop, calls=%fused_computation.63 | loop fusion | flops 3932160 | bytes 13123584 | tf_op jit(solution)/shard_map/convert_element_type | solution.py:79
  27.2 2.2 %all-gather.2.cloned.1.call-done = bf16[2048,256]{1,0:T(8,128)(2,1)} async-done(((bf16[512,256]{1,0:T(8,128)(2,1)}), bf16[2048,256]{1,0:T(8,128)(2,1)}) %all-gather.2.cloned.1.call-update) | async-done | bytes 1048592 | tf_op jit(solution)/shard_map/all_gather | solution.py:56
  29.5 4.0 %fusion.2 = (f32[2048]{0:T(1024)S(1)}, f32[2048,2048]{1,0:T(8,128)S(1)}) fusion(s32[2048]{0:T(1024)S(1)} %broadcast_add_fusion, bf16[2048,128]{1,0:T(8,128)(2,1)S(1)} %reshape.53, bf16[2048,256]{1,0:T(8,128)(2,1)} %all-gather.2.cloned.1.call-done), kind=kOutput, calls=%fused_computation.5 | convolution fusion | flops 1090516992 | bytes 17842176 | tf_op jit(solution)/shard_map/dot_general | solution.py:19
  33.5 4.4 %fusion = f32[2048]{0:T(1024)S(1)} fusion(f32[2048,2048]{1,0:T(8,128)S(1)} %get-tuple-element.19, f32[2048]{0:T(1024)S(1)} %broadcast_maximum_fusion, s32[2048]{0:T(1024)S(1)} %broadcast_add_fusion), kind=kLoop, calls=%fused_computation.3 | loop fusion | flops 20969472 | bytes 16801792 | tf_op jit(solution)/shard_map/reduce_sum | solution.py:24
  38.0 4.9 %fusion.8 = f32[2048,128]{1,0:T(8,128)S(1)} fusion(f32[2048,2048]{1,0:T(8,128)S(1)} %get-tuple-element.19, f32[2048]{0:T(1024)S(1)} %broadcast_maximum_fusion, s32[2048]{0:T(1024)S(1)} %broadcast_add_fusion, bf16[2048,256]{1,0:T(8,128)(2,1)S(1)} %copy-done.4, f32[2048]{0:T(1024)S(1)} %fusion), kind=kOutput, calls=%fused_computation.15 | convolution fusion | flops 1094975488 | bytes 18374656 | tf_op jit(solution)/shard_map/dot_general | solution.py:25
  42.9 0.9 %fusion.7 = bf16[2048,128]{1,0:T(8,128)(2,1)S(1)} fusion(f32[2048,128]{1,0:T(8,128)S(1)} %fusion.8, bf16[2048,640]{0,1:T(8,128)(2,1)S(1)} %get-tuple-element.12, bf16[512,128]{1,0:T(8,128)(2,1)S(1)} %copy-done.2, bf16[128,128]{1,0:T(8,128)(2,1)S(1)} %get-tuple-element.16), kind=kOutput, calls=%fused_computation.14 | convolution fusion | flops 336396288 | bytes 4358144 | tf_op jit(solution)/shard_map/dot_general | solution.py:80
  43.8 0.3 convolution_convert_fusion
  44.2 0.9 %multiply_reduce_fusion = (f32[2048]{0:T(1024)S(1)}, f32[2048,640]{0,1:T(8,128)S(1)}) fusion(f32[2048,640]{0,1:T(8,128)S(1)} %bitcast.22, bf16[2048,128]{1,0:T(8,128)(2,1)S(1)} %fusion.7, bf16[512,128]{1,0:T(8,128)(2,1)S(1)} %copy-done.2, bf16[128,128]{1,0:T(8,128)(2,1)S(1)} %get-tuple-element.16), kind=kOutput, calls=%fused_computation.8 | convolution fusion | flops 338491392 | bytes 11182080 | tf_op jit(solution)/shard_map/dot_general | solution.py:82
  45.0 0.2 copy-done.1
  45.2 0.4 fusion.11
  45.6 0.7 copy.13
  46.3 0.0 reduce-scatter.4.cloned.1.call-update
  46.3 1.1 %reshape.54 = bf16[512,512]{1,0:T(8,128)(2,1)} reshape(bf16[2048,128]{1,0:T(8,128)(2,1)S(1)} %fusion.7) | data formatting | bytes 1048576 | tf_op jit(solution)/shard_map/reshape | solution.py:99
  47.4 18.6 %reduce-scatter.4.cloned.1.call-done = bf16[32,256]{1,0:T(8,128)(2,1)} async-done(((bf16[128,256]{1,0:T(8,128)(2,1)}), bf16[32,256]{1,0:T(8,128)(2,1)}) %reduce-scatter.4.cloned.1.call-update) | async-done | bytes 16400
  66.0 0.8 %copy.14 = bf16[32,256]{0,1:T(8,128)(2,1)S(1)} copy(bf16[32,256]{1,0:T(8,128)(2,1)} %reduce-scatter.4.cloned.1.call-done) | data formatting | bytes 32768
  66.9 0.7 copy.11
  67.6 0.7 copy.12
  (21 shorter events, 0.1 us)
Async XLA Ops:
  7.2 22.3 %all-gather.2.cloned.1.call-start = ((), (), s32[]{:S(2)}) async-start(), calls=%async_computation.1 | async-start | bytes 1310720 | tf_op jit(solution)/shard_map/all_gather | solution.py:56
  9.1 0.7 copy-start.3
  9.8 56.2 %reduce-scatter.4.cloned.1.call-start = ((), (), s32[]{:S(2)}) async-start(), calls=%async_computation.2 | async-start | bytes 81920
  21.0 8.4 %copy-start = (bf16[2048,128]{1,0:T(8,128)(2,1)}, bf16[2048,128]{1,0:T(8,128)(2,1)S(1)}, u32[]{:S(2)}) copy-start(bf16[2048,128]{1,0:T(8,128)(2,1)S(1)} %reshape.53) | copy-start | bytes 1572868
  33.5 4.5 %copy-start.4 = (bf16[2048,256]{1,0:T(8,128)(2,1)S(1)}, bf16[2048,256]{1,0:T(8,128)(2,1)}, u32[]{:S(2)}) copy-start(bf16[2048,256]{1,0:T(8,128)(2,1)} %all-gather.2.cloned.1.call-done) | copy-start | bytes 3145732
  33.5 10.6 %slice-start = ((s8[5242880]{0:T(1024)(128)(4,1)}), s8[4194304]{0:T(1024)(128)(4,1)S(1)}, s32[]{:S(2)}) async-start(s8[5242880]{0:T(1024)(128)(4,1)} %bitcast.21), calls=%async_computation.3 | async-start | bytes 8388608
  37.9 4.9 %copy-start.2 = (bf16[512,128]{1,0:T(8,128)(2,1)S(1)}, bf16[512,128]{1,0:T(8,128)(2,1)}, u32[]{:S(2)}) copy-start(bf16[512,128]{1,0:T(8,128)(2,1)} %param.6) | copy-start | bytes 393220
  38.0 6.2 %slice-start.1 = ((s8[5242880]{0:T(1024)(128)(4,1)}), s8[1048576]{0:T(1024)(128)(4,1)S(1)}, s32[]{:S(2)}) async-start(s8[5242880]{0:T(1024)(128)(4,1)} %bitcast.21), calls=%async_computation.4 | async-start | bytes 2097152
  44.2 1.0 %copy-start.1 = (bf16[2048,128]{1,0:T(8,128)(2,1)S(1)}, bf16[2048,128]{1,0:T(8,128)(2,1)}, u32[]{:S(2)}) copy-start(bf16[2048,128]{1,0:T(8,128)(2,1)} %copy-done) | copy-start | bytes 1572868
Sparse Core Ops, SparseCore 0:
  9.9 19.4 all-gather.1
  46.5 19.5 reduce-scatter.3
where the time goes:
time: 75.5 us; the launch traced here: 75.1 us
  waiting for transfers between devices  20.8 us (28%)
  matrix products  14.7 us (19%)
  between operations  14.3 us (19%)
  other arithmetic  9.98 us (13%)
  local copies, waits for them, and re-layouts  9 us (12%)
  blocking collectives  6.19 us (8%)
    unnamed x3, waiting for transfers between devices  18.6 us
    all_gather x1, blocking collectives, body(): beacons = lax.all_gather(beacon_rows, 'seq', axis=0, tiled=True)  6.19 us
    dot_general x1, matrix products, attend_block(): jnp.dot(weights.astype(jnp.bfloat16), piece[:, head_size:], preferred_ele...  4.88 us
    unnamed x19, local copies, waits for them, and re-layouts  4.76 us
    reduce_sum x1, other arithmetic, attend_block(): total_weight = jnp.sum(weights, axis=1)  4.43 us
    dot_general x1, matrix products, attend_block(): jnp.dot(query_rows, piece[:, :head_size].T, preferred_element_type=jnp.fl...  4 us
    convert_element_type x1, other arithmetic, body(): probs_low = student_probs.astype(jnp.bfloat16)  3.24 us
    all_gather x1, waiting for transfers between devices, body(): lax.all_gather(joined, 'seq', axis=0, tiled=True)  2.21 us
  transfers between devices with their start and end apart: 2, of which 2 were waited for; matrix products, arithmetic and copies ran while one was open for 16% of the time, Pallas kernels for 0%

commit v1 on v0

v1 whole, which is shorter than its diff:
```python
import functools
import math

import jax
import jax.numpy as jnp
from jax import lax
from jax.experimental import pallas as pl
from jax.experimental.pallas import tpu as pltpu
from jax.sharding import PartitionSpec as P

NEG = -1e30
MESH = pl.DeviceIdType.MESH


def dot_nt(a, b):
    return lax.dot_general(a, b, (((1,), (1,)), ((), ())), preferred_element_type=jnp.float32)


def dot_tn(a, b):
    return lax.dot_general(a, b, (((0,), (0,)), ((), ())), preferred_element_type=jnp.float32)


def dot_nn(a, b):
    return jnp.dot(a, b, preferred_element_type=jnp.float32)


def wide(a, width):
    reps = width // a.shape[1]
    return a if reps == 1 else jnp.concatenate([a] * reps, axis=1)


def with_ones(v):
    return jnp.concatenate([v, jnp.ones_like(v)], axis=1)


def kernel(
    n,
    starts_ref,
    q_ref,
    k_ref,
    v_ref,
    gap_ref,
    gk_ref,
    gv_ref,
    k_all,
    v_all,
    beac,
    state_m,
    state_acc,
    student,
    probs,
    sum_k,
    sum_v,
    stage,
    landed,
    k_send,
    v_send,
    k_fwd,
    v_fwd,
    k_recv,
    v_recv,
    b_send,
    b_recv,
    g_send,
    g_recv,
):
    me = lax.axis_index("seq")
    chip = me // 2
    core = me % 2
    partner = me + 1 - 2 * core
    chips = n // 2
    tok, dim = k_ref.shape
    heads = q_ref.shape[1] // dim
    count = starts_ref.shape[0]
    half = tok // 2
    scaling = dim ** (-0.5)
    fold = scaling * math.log2(math.e)

    def remote(src, dst, send, recv, target):
        return pltpu.make_async_remote_copy(
            src_ref=src,
            dst_ref=dst,
            send_sem=send,
            recv_sem=recv,
            device_id={"seq": target},
            device_id_type=MESH,
        )

    barrier = pltpu.get_barrier_semaphore()
    for other in range(1, n):
        pl.semaphore_signal(
            barrier, inc=1, device_id={"seq": lax.rem(me + other, n)}, device_id_type=MESH
        )

    pos = lax.broadcasted_iota(jnp.int32, (8, tok), 1)
    rank = jnp.zeros((8, tok), jnp.int32)
    for b in range(1, count):
        rank = rank + (pos >= starts_ref[b]).astype(jnp.int32)
    rank = jnp.concatenate([rank] * (count // 8), axis=0)
    member = (rank == lax.broadcasted_iota(jnp.int32, (count, tok), 0)).astype(jnp.float32)
    counts = jnp.sum(member, axis=1, keepdims=True)
    joined = jnp.concatenate([k_ref[...], v_ref[...]], axis=1)
    pooled = dot_nn(member.astype(jnp.bfloat16), joined)
    beac[pl.ds(me, 1)] = (pooled / counts).astype(jnp.bfloat16)[None]

    pl.semaphore_wait(barrier, n - 1)

    def kv_copies(src_k, src_v, slot, sk, sv, target):
        return (
            remote(src_k, k_all.at[slot], sk, k_recv.at[slot], target),
            remote(src_v, v_all.at[slot], sv, v_recv.at[slot], target),
        )

    def direct(c):
        return kv_copies(k_ref, v_ref, me, k_send.at[c], v_send.at[c], 2 * c + core)

    def to_partner():
        return kv_copies(k_ref, v_ref, me, k_send.at[chips], v_send.at[chips], partner)

    def forward(c):
        slot = 2 * c + core
        return kv_copies(k_all.at[slot], v_all.at[slot], slot, k_fwd.at[c], v_fwd.at[c], partner)

    def beacon_copy(s):
        return remote(beac.at[me], beac.at[me], b_send.at[s], b_recv.at[me], s)

    def beacon_arrival(s):
        return remote(beac.at[s], beac.at[s], b_send.at[s], b_recv.at[s], partner)

    def grad_copy(s):
        return remote(stage.at[s], landed.at[me], g_send.at[s], g_recv.at[me], s)

    def grad_arrival(d):
        return remote(stage.at[d], landed.at[d], g_send.at[d], g_recv.at[d], partner)

    for c in range(chips):

        @pl.when(c > chip)
        def _():
            for copy in direct(c):
                copy.start()

    for s in range(1, n):

        @pl.when(s > me)
        def _():
            beacon_copy(s).start()

    @pl.when(core == 0)
    def _():
        for copy in to_partner():
            copy.start()

    def own_tile(h, carry):
        cols = pl.ds(pl.multiple_of(h * dim, dim), dim)
        for part in range(2):
            keys = half * (part + 1)
            rows = pl.ds(part * half, half)
            s = dot_nt(q_ref[rows, cols], k_ref[:keys])
            row_pos = lax.broadcasted_iota(jnp.int32, (half, keys), 0) + part * half
            s = jnp.where(lax.broadcasted_iota(jnp.int32, (half, keys), 1) <= row_pos, s, NEG)
            m = jnp.broadcast_to(jnp.max(s, axis=1, keepdims=True), (half, dim))
            p = jnp.exp2((s - wide(m, keys)) * fold).astype(jnp.bfloat16)
            state_m[h, rows] = m
            state_acc[h, rows] = dot_nn(p, with_ones(v_ref[:keys]))
        return carry

    lax.fori_loop(0, heads, own_tile, 0)

    for s in range(n - 1):

        @pl.when(s < me)
        def _():
            beacon_arrival(s).wait_recv()

        @pl.when(s > me)
        def _():
            beac[s] = jnp.zeros((count, 2 * dim), jnp.bfloat16)

    @pl.when(me < n - 1)
    def _():
        beac[n - 1] = jnp.zeros((count, 2 * dim), jnp.bfloat16)

    nb = n * count

    def student_tile(h, carry):
        cols = pl.ds(pl.multiple_of(h * dim, dim), dim)
        rows = beac[...].reshape(nb, 2 * dim)
        s = dot_nt(q_ref[:, cols], rows[:, :dim])
        s = jnp.where(lax.broadcasted_iota(jnp.int32, (tok, nb), 1) < me * count, s, NEG)
        m_own = state_m[h]
        m = jnp.maximum(m_own, jnp.broadcast_to(jnp.max(s, axis=1, keepdims=True), (tok, dim)))
        w = jnp.exp2((s - wide(m, nb)) * fold)
        acc = state_acc[h] * wide(jnp.exp2((m_own - m) * fold), 2 * dim)
        acc = acc + dot_nn(w.astype(jnp.bfloat16), with_ones(rows[:, dim:]))
        inverse = 1.0 / acc[:, dim:]
        student[h] = acc[:, :dim] * inverse
        probs[h] = (w * wide(inverse, nb)).astype(jnp.bfloat16)
        return carry

    lax.fori_loop(0, heads, student_tile, 0)

    def fold_block(slot):
        def tile(h, carry):
            cols = pl.ds(pl.multiple_of(h * dim, dim), dim)
            s = dot_nt(q_ref[:, cols], k_all[slot])
            m_old = state_m[h]
            m = jnp.maximum(m_old, jnp.broadcast_to(jnp.max(s, axis=1, keepdims=True), (tok, dim)))
            p = jnp.exp2((s - wide(m, tok)) * fold).astype(jnp.bfloat16)
            state_m[h] = m
            state_acc[h] = state_acc[h] * wide(jnp.exp2((m_old - m) * fold), 2 * dim) + dot_nn(
                p, with_ones(v_all[slot])
            )
            return carry

        lax.fori_loop(0, heads, tile, 0)

    @pl.when(core == 1)
    def _():
        for copy in kv_copies(
            k_ref, v_ref, me - 1, k_send.at[chips], v_send.at[chips], partner
        ):
            copy.wait_recv()

    def relay(c, carry):
        arrival = kv_copies(
            k_ref, v_ref, 2 * c + core, k_send.at[c], v_send.at[c], partner
        )
        passed = forward(c)
        for a, f in zip(arrival, passed):
            a.wait_recv()
            f.start()
        return carry

    def direct_block(c, carry):
        fold_block(2 * c + core)
        return carry

    @pl.when(core == 1)
    def _():
        fold_block(me - 1)

    lax.fori_loop(0, chip, relay, 0)
    lax.fori_loop(0, chip, direct_block, 0)

    def passed_block(c, carry):
        slot = 2 * c + 1 - core
        for a in kv_copies(k_ref, v_ref, slot, k_send.at[c], v_send.at[c], partner):
            a.wait_recv()
        fold_block(slot)
        return carry

    lax.fori_loop(0, chip, passed_block, 0)

    sum_k[...] = jnp.zeros_like(sum_k)
    sum_v[...] = jnp.zeros_like(sum_v)

    def grad_tile(h, carry):
        cols = pl.ds(pl.multiple_of(h * dim, dim), dim)
        values = beac[...].reshape(nb, 2 * dim)[:, dim:]
        out = student[h]
        gap = (out - state_acc[h, :, :dim] / state_acc[h, :, dim:]).astype(jnp.bfloat16)
        gap_ref[:, cols] = gap
        row_dot = jnp.sum(out * gap.astype(jnp.float32), axis=1, keepdims=True)
        low = probs[h]
        d = low.astype(jnp.float32) * (dot_nt(gap, values) - row_dot)
        sum_k[...] += dot_tn(d.astype(jnp.bfloat16), q_ref[:, cols])
        sum_v[...] += dot_tn(low, gap)
        return carry

    lax.fori_loop(0, heads, grad_tile, 0)

    terms = jnp.concatenate([sum_k[...] * scaling, sum_v[...]], axis=1)
    stage[...] = terms.astype(jnp.bfloat16).reshape(n, count, 2 * dim)
    for s in range(n - 1):

        @pl.when(s < me)
        def _():
            grad_copy(s).start()

    gk_ref[...] = jnp.zeros_like(gk_ref)
    gv_ref[...] = jnp.zeros_like(gv_ref)
    for d in range(1, n):

        @pl.when(d > me)
        def _():
            grad_arrival(d).wait_recv()
            part = landed[d].astype(jnp.float32)
            gk_ref[...] += part[:, :dim]
            gv_ref[...] += part[:, dim:]

    for c in range(chips):

        @pl.when(c > chip)
        def _():
            for copy in direct(c):
                copy.wait_send()

        @pl.when(c < chip)
        def _():
            for copy in forward(c):
                copy.wait_send()

    for s in range(n):

        @pl.when(s > me)
        def _():
            beacon_copy(s).wait_send()

        @pl.when(s < me)
        def _():
            grad_copy(s).wait_send()

    @pl.when(core == 0)
    def _():
        for copy in to_partner():
            copy.wait_send()


def body(n, queries, teacher_keys, teacher_values, beacon_starts):
    tok, dim = teacher_keys.shape
    heads = queries.shape[1] // dim
    count = beacon_starts.shape[0]
    chips = n // 2
    vmem = pl.BlockSpec(memory_space=pltpu.VMEM)
    dma = pltpu.SemaphoreType.DMA
    return pl.pallas_call(
        functools.partial(kernel, n),
        out_shape=(
            jax.ShapeDtypeStruct(queries.shape, jnp.bfloat16),
            jax.ShapeDtypeStruct((count, dim), jnp.float32),
            jax.ShapeDtypeStruct((count, dim), jnp.float32),
        ),
        in_specs=[pl.BlockSpec(memory_space=pltpu.SMEM), vmem, vmem, vmem],
        out_specs=(vmem, vmem, vmem),
        scratch_shapes=[
            pltpu.VMEM((n, tok, dim), jnp.bfloat16),
            pltpu.VMEM((n, tok, dim), jnp.bfloat16),
            pltpu.VMEM((n, count, 2 * dim), jnp.bfloat16),
            pltpu.VMEM((heads, tok, dim), jnp.float32),
            pltpu.VMEM((heads, tok, 2 * dim), jnp.float32),
            pltpu.VMEM((heads, tok, dim), jnp.float32),
            pltpu.VMEM((heads, tok, n * count), jnp.bfloat16),
            pltpu.VMEM((n * count, dim), jnp.float32),
            pltpu.VMEM((n * count, dim), jnp.float32),
            pltpu.VMEM((n, count, 2 * dim), jnp.bfloat16),
            pltpu.VMEM((n, count, 2 * dim), jnp.bfloat16),
            dma((chips + 1,)),
            dma((chips + 1,)),
            dma((chips,)),
            dma((chips,)),
            dma((n,)),
            dma((n,)),
            dma((n,)),
            dma((n,)),
            dma((n,)),
            dma((n,)),
        ],
        compiler_params=pltpu.CompilerParams(collective_id=0, has_side_effects=True),
    )(beacon_starts, queries, teacher_keys, teacher_values)


def solution(mesh):
    spec = P(("doc", "seq"), None)
    return jax.shard_map(
        functools.partial(body, mesh.shape["seq"]),
        mesh=mesh,
        in_specs=(spec, spec, spec, P(("doc", "seq"))),
        out_specs=(spec, spec, spec),
        check_vma=False,
    )
```

time: 75.5 us -> 32.7 us (0.43)
  Pallas kernels: 0 us -> 28.6 us
  waiting for transfers between devices: 20.8 us -> 0 us
  matrix products: 14.7 us -> 0 us
  between operations: 14.3 us -> 0.65 us
  other arithmetic: 9.98 us -> 0 us
  blocking collectives: 6.19 us -> 0 us
  local copies, waits for them, and re-layouts: 9 us -> 3.21 us
    pallas_call x0 -> x1, Pallas kernels: none -> 28.6 us  [body(): pl.pallas_call(functools.partial(kernel, n), out_shape=(jax.ShapeDtypeStr...]
    unnamed x3 -> x0, waiting for transfers between devices: 18.6 us -> none
    dot_general x8 -> x0, matrix products: 14.7 us -> none  [the longest x1 4.88 us: attend_block(): jnp.dot(weights.astype(jnp.bfloat16), piece[:, head_size:], preferred_ele...]
    all_gather x1 -> x0, blocking collectives: 6.19 us -> none  [body(): beacons = lax.all_gather(beacon_rows, 'seq', axis=0, tiled=True)]
    reduce_sum x3 -> x0, other arithmetic: 6.01 us -> none  [the longest x1 4.43 us: attend_block(): total_weight = jnp.sum(weights, axis=1)]
    convert_element_type x1 -> x0, other arithmetic: 3.24 us -> none  [body(): probs_low = student_probs.astype(jnp.bfloat16)]
    reshape x2 -> x0, local copies, waits for them, and re-layouts: 2.56 us -> none  [the longest x1 1.45 us: body(): query_rows = queries.reshape(row_count, head_size)]
    all_gather x1 -> x0, waiting for transfers between devices: 2.21 us -> none  [body(): lax.all_gather(joined, 'seq', axis=0, tiled=True)]
  transfers between devices with their start and end apart: 2 -> 0, of which waited for: 2 -> 0; matrix products, arithmetic and copies ran while one was open for 16% -> 0% of each run, Pallas kernels for 0% -> 0%
where the time goes in v1:
time: 32.7 us; the launch traced here: 32.4 us
  Pallas kernels  28.6 us (87%)
  local copies, waits for them, and re-layouts  3.21 us (10%)
  between operations  0.65 us (2%)
    pallas_call x1, Pallas kernels, body(): pl.pallas_call(functools.partial(kernel, n), out_shape=(jax.ShapeDtypeStr...  28.6 us
    unnamed x7, local copies, waits for them, and re-layouts  3.21 us

profile of v1, /device:TPU:0, one launch (start us, length us, event | category | flops | bytes accessed | tf_op | source)
XLA Modules:
  0.0 32.4 jit_solution(17312379717790063940)
XLA Ops:
  0.6 28.6 %shard_map.67 = (bf16[512,512]{1,0:T(8,128)(2,1)}, f32[32,128]{1,0:T(8,128)}, f32[32,128]{1,0:T(8,128)}) custom-call(s32[32]{0:T(128)} %starts_ref.1, bf16[512,512]{1,0:T(8,128)(2,1)} %q_ref.1, bf16[512,128]{1,0:T(8,128)(2,1)} %k_ref.1, bf16[512,128]{1,0:T(8,128)(2,1)} %v_ref.1), custom_call_target="tpu_custom_call" | custom-call | tf_op jit(solution)/shard_map/pallas_call | solution.py:327
  29.2 0.0 copy-start.1
  29.2 1.9 %copy.10 = bf16[512,512]{1,0:T(8,128)(2,1)} copy(bf16[512,512]{1,0:T(8,128)(2,1)} %get-tuple-element.6) | data formatting | bytes 1048576
  31.1 0.0 copy-done.1
  31.1 0.0 copy-start
  31.1 0.6 %copy.11 = f32[32,128]{1,0:T(8,128)} copy(f32[32,128]{1,0:T(8,128)S(1)} %copy-done.1) | data formatting | bytes 32768
  31.7 0.1 copy-done
  31.8 0.6 %copy.12 = f32[32,128]{1,0:T(8,128)} copy(f32[32,128]{1,0:T(8,128)S(1)} %copy-done) | data formatting | bytes 32768
Async XLA Ops:
  29.2 1.9 %copy-start.1 = (f32[32,128]{1,0:T(8,128)S(1)}, f32[32,128]{1,0:T(8,128)}, u32[]{:S(2)}) copy-start(f32[32,128]{1,0:T(8,128)} %get-tuple-element.7) | copy-start | bytes 49156
  31.1 0.7 %copy-start = (f32[32,128]{1,0:T(8,128)S(1)}, f32[32,128]{1,0:T(8,128)}, u32[]{:S(2)}) copy-start(f32[32,128]{1,0:T(8,128)} %get-tuple-element.8) | copy-start | bytes 49156

commit v2 on v1

v2 whole, which is shorter than its diff:
```python
import functools
import math

import jax
import jax.numpy as jnp
from jax import lax
from jax.experimental import pallas as pl
from jax.experimental.pallas import tpu as pltpu
from jax.sharding import PartitionSpec as P

NEG = -1e30
CHUNKS = 2
MESH = pl.DeviceIdType.MESH


def dot_nt(a, b):
    return lax.dot_general(a, b, (((1,), (1,)), ((), ())), preferred_element_type=jnp.float32)


def dot_tn(a, b):
    return lax.dot_general(a, b, (((0,), (0,)), ((), ())), preferred_element_type=jnp.float32)


def dot_nn(a, b):
    return jnp.dot(a, b, preferred_element_type=jnp.float32)


def wide(a, width):
    reps = width // a.shape[1]
    return a if reps == 1 else jnp.concatenate([a] * reps, axis=1)


def with_ones(v):
    return jnp.concatenate([v, jnp.ones_like(v)], axis=1)


def kernel(
    n,
    starts_hbm,
    q_hbm,
    k_hbm,
    v_hbm,
    gap_ref,
    gk_ref,
    gv_ref,
    starts_ref,
    q_ref,
    kv,
    beac,
    state_m,
    state_acc,
    student,
    probs,
    stage,
    landed,
    load,
    kv_send,
    kv_fwd,
    kv_recv,
    b_send,
    b_recv,
    g_send,
    g_recv,
):
    me = lax.axis_index("seq")
    chip = me // 2
    core = me % 2
    partner = me + 1 - 2 * core
    chips = n // 2
    tok, dim = k_hbm.shape
    heads = q_hbm.shape[1] // dim
    count = starts_ref.shape[0]
    nb = n * count
    half = tok // 2
    piece = tok // CHUNKS
    scaling = dim ** (-0.5)
    fold = scaling * math.log2(math.e)

    def remote(src, dst, send, recv, target):
        return pltpu.make_async_remote_copy(
            src_ref=src,
            dst_ref=dst,
            send_sem=send,
            recv_sem=recv,
            device_id={"seq": target},
            device_id_type=MESH,
        )

    barrier = pltpu.get_barrier_semaphore()
    for other in range(1, n):
        pl.semaphore_signal(
            barrier, inc=1, device_id={"seq": lax.rem(me + other, n)}, device_id_type=MESH
        )
    loads = (
        pltpu.make_async_copy(k_hbm, kv.at[me, :, pl.ds(0, dim)], load.at[0]),
        pltpu.make_async_copy(v_hbm, kv.at[me, :, pl.ds(dim, dim)], load.at[1]),
        pltpu.make_async_copy(q_hbm, q_ref, load.at[2]),
        pltpu.make_async_copy(starts_hbm, starts_ref, load.at[3]),
    )
    for copy in loads:
        copy.start()

    def part(i):
        return pl.ds(i * piece, piece)

    def direct(c, i):
        here = kv.at[me, part(i)]
        return remote(here, here, kv_send.at[c, i], kv_recv.at[me, i], 2 * c + core)

    def to_partner(i):
        here = kv.at[me, part(i)]
        return remote(here, here, kv_send.at[chips, i], kv_recv.at[me, i], partner)

    def arrival(slot, i):
        there = kv.at[slot, part(i)]
        return remote(there, there, kv_send.at[chips, i], kv_recv.at[slot, i], partner)

    def forward(c, i):
        slot = 2 * c + core
        there = kv.at[slot, part(i)]
        return remote(there, there, kv_fwd.at[c, i], kv_recv.at[slot, i], partner)

    def beacon_copy(s):
        return remote(beac.at[me], beac.at[me], b_send.at[s], b_recv.at[me], s)

    def beacon_arrival(s):
        return remote(beac.at[s], beac.at[s], b_send.at[s], b_recv.at[s], partner)

    def grad_copy(s):
        return remote(stage.at[s], landed.at[me], g_send.at[s], g_recv.at[me], s)

    def grad_arrival(d):
        return remote(stage.at[d], landed.at[d], g_send.at[d], g_recv.at[d], partner)

    loads[0].wait()
    loads[1].wait()
    pl.semaphore_wait(barrier, n - 1)

    for c in range(1, chips):

        @pl.when(c > chip)
        def _():
            for i in range(CHUNKS):
                direct(c, i).start()

    @pl.when(core == 0)
    def _():
        for i in range(CHUNKS):
            to_partner(i).start()

    loads[3].wait()
    pos = lax.broadcasted_iota(jnp.int32, (8, tok), 1)
    rank = jnp.zeros((8, tok), jnp.int32)
    for b in range(1, count):
        rank = rank + (pos >= starts_ref[b]).astype(jnp.int32)
    rank = jnp.concatenate([rank] * (count // 8), axis=0)
    member = (rank == lax.broadcasted_iota(jnp.int32, (count, tok), 0)).astype(jnp.float32)
    inverse_count = 1.0 / jnp.sum(member, axis=1, keepdims=True)
    pooled = dot_nn(member.astype(jnp.bfloat16), kv[me])
    beac[pl.ds(me, 1)] = (pooled * inverse_count).astype(jnp.bfloat16)[None]

    for s in range(1, n):

        @pl.when(s > me)
        def _():
            beacon_copy(s).start()
            beac[s] = jnp.zeros((count, 2 * dim), jnp.bfloat16)

    loads[2].wait()

    for h in range(heads):
        cols = pl.ds(h * dim, dim)
        for side in range(2):
            keys = half * (side + 1)
            rows = pl.ds(side * half, half)
            s = dot_nt(q_ref[rows, cols], kv[me, :keys, :dim])
            row_pos = lax.broadcasted_iota(jnp.int32, (half, keys), 0) + side * half
            s = jnp.where(lax.broadcasted_iota(jnp.int32, (half, keys), 1) <= row_pos, s, NEG)
            m = jnp.broadcast_to(jnp.max(s, axis=1, keepdims=True), (half, dim))
            p = jnp.exp2((s - wide(m, keys)) * fold).astype(jnp.bfloat16)
            state_m[h, rows] = m
            state_acc[h, rows] = dot_nn(p, with_ones(kv[me, :keys, dim:]))

    for s in range(n - 1):

        @pl.when(s < me)
        def _():
            beacon_arrival(s).wait_recv()

    beacons = beac[...].reshape(nb, 2 * dim)
    for h in range(heads):
        cols = pl.ds(h * dim, dim)
        s = dot_nt(q_ref[:, cols], beacons[:, :dim])
        s = jnp.where(lax.broadcasted_iota(jnp.int32, (tok, nb), 1) < me * count, s, NEG)
        m_own = state_m[h]
        m = jnp.maximum(m_own, jnp.broadcast_to(jnp.max(s, axis=1, keepdims=True), (tok, dim)))
        w = jnp.exp2((s - wide(m, nb)) * fold)
        acc = state_acc[h] * wide(jnp.exp2((m_own - m) * fold), 2 * dim)
        acc = acc + dot_nn(w.astype(jnp.bfloat16), with_ones(beacons[:, dim:]))
        inverse = 1.0 / acc[:, dim:]
        student[h] = acc[:, :dim] * inverse
        probs[h] = (w * wide(inverse, nb)).astype(jnp.bfloat16)

    def fold_block(slot, first, keys):
        for h in range(heads):
            cols = pl.ds(h * dim, dim)
            for side in range(2):
                rows = pl.ds(side * half, half)
                s = dot_nt(q_ref[rows, cols], kv[slot, pl.ds(first, keys), :dim])
                m_old = state_m[h, rows]
                m = jnp.maximum(
                    m_old, jnp.broadcast_to(jnp.max(s, axis=1, keepdims=True), (half, dim))
                )
                p = jnp.exp2((s - wide(m, keys)) * fold).astype(jnp.bfloat16)
                state_m[h, rows] = m
                state_acc[h, rows] = state_acc[h, rows] * wide(
                    jnp.exp2((m_old - m) * fold), 2 * dim
                ) + dot_nn(p, with_ones(kv[slot, pl.ds(first, keys), dim:]))

    @pl.when(core == 1)
    def _():
        for i in range(CHUNKS):
            arrival(me - 1, i).wait_recv()
        fold_block(me - 1, 0, tok)

    def direct_block(c, carry):
        for i in range(CHUNKS):
            arrival(2 * c + core, i).wait_recv()
            forward(c, i).start()
            fold_block(2 * c + core, i * piece, piece)
        return carry

    lax.fori_loop(0, chip, direct_block, 0)

    def passed_block(c, carry):
        slot = 2 * c + 1 - core
        for i in range(CHUNKS):
            arrival(slot, i).wait_recv()
        fold_block(slot, 0, tok)
        return carry

    lax.fori_loop(0, chip, passed_block, 0)

    values = beac[...].reshape(nb, 2 * dim)[:, dim:]
    sum_k = jnp.zeros((nb, dim), jnp.float32)
    sum_v = jnp.zeros((nb, dim), jnp.float32)
    for h in range(heads):
        cols = pl.ds(h * dim, dim)
        out = student[h]
        gap = (out - state_acc[h, :, :dim] / state_acc[h, :, dim:]).astype(jnp.bfloat16)
        gap_ref[:, cols] = gap
        row_dot = jnp.sum(out * gap.astype(jnp.float32), axis=1, keepdims=True)
        low = probs[h]
        d = low.astype(jnp.float32) * (dot_nt(gap, values) - row_dot)
        sum_k += dot_tn(d.astype(jnp.bfloat16), q_ref[:, cols])
        sum_v += dot_tn(low, gap)

    terms = jnp.concatenate([sum_k * scaling, sum_v], axis=1)
    stage[...] = terms.astype(jnp.bfloat16).reshape(n, count, 2 * dim)
    for s in range(n - 1):

        @pl.when(s < me)
        def _():
            grad_copy(s).start()

    gk_ref[...] = jnp.zeros_like(gk_ref)
    gv_ref[...] = jnp.zeros_like(gv_ref)
    for d in range(1, n):

        @pl.when(d > me)
        def _():
            grad_arrival(d).wait_recv()
            term = landed[d].astype(jnp.float32)
            gk_ref[...] += term[:, :dim]
            gv_ref[...] += term[:, dim:]

    for c in range(chips):

        @pl.when(c > chip)
        def _():
            for i in range(CHUNKS):
                direct(c, i).wait_send()

        @pl.when(c < chip)
        def _():
            for i in range(CHUNKS):
                forward(c, i).wait_send()

    for s in range(n):

        @pl.when(s > me)
        def _():
            beacon_copy(s).wait_send()

        @pl.when(s < me)
        def _():
            grad_copy(s).wait_send()

    @pl.when(core == 0)
    def _():
        for i in range(CHUNKS):
            to_partner(i).wait_send()


def hand_out(gap, gk, gv, gap_out, gk_out, gv_out, sems):
    copies = [
        pltpu.make_async_copy(src, dst, sems.at[i])
        for i, (src, dst) in enumerate(((gap, gap_out), (gk, gk_out), (gv, gv_out)))
    ]
    for copy in copies:
        copy.start()
    for copy in copies:
        copy.wait()


def body(n, queries, teacher_keys, teacher_values, beacon_starts):
    tok, dim = teacher_keys.shape
    heads = queries.shape[1] // dim
    count = beacon_starts.shape[0]
    chips = n // 2
    vmem = pl.BlockSpec(memory_space=pltpu.VMEM)
    hbm = pl.BlockSpec(memory_space=pltpu.HBM)
    dma = pltpu.SemaphoreType.DMA
    out_shape = (
        jax.ShapeDtypeStruct(queries.shape, jnp.bfloat16),
        jax.ShapeDtypeStruct((count, dim), jnp.float32),
        jax.ShapeDtypeStruct((count, dim), jnp.float32),
    )
    arrays = [
        pltpu.with_memory_space_constraint(a, pltpu.HBM)
        for a in (beacon_starts, queries, teacher_keys, teacher_values)
    ]
    results = pl.pallas_call(
        functools.partial(kernel, n),
        out_shape=out_shape,
        in_specs=[hbm, hbm, hbm, hbm],
        out_specs=(vmem, vmem, vmem),
        scratch_shapes=[
            pltpu.SMEM((count,), jnp.int32),
            pltpu.VMEM(queries.shape, jnp.bfloat16),
            pltpu.VMEM((n, tok, 2 * dim), jnp.bfloat16),
            pltpu.VMEM((n, count, 2 * dim), jnp.bfloat16),
            pltpu.VMEM((heads, tok, dim), jnp.float32),
            pltpu.VMEM((heads, tok, 2 * dim), jnp.float32),
            pltpu.VMEM((heads, tok, dim), jnp.float32),
            pltpu.VMEM((heads, tok, n * count), jnp.bfloat16),
            pltpu.VMEM((n, count, 2 * dim), jnp.bfloat16),
            pltpu.VMEM((n, count, 2 * dim), jnp.bfloat16),
            dma((4,)),
            dma((chips + 1, CHUNKS)),
            dma((chips, CHUNKS)),
            dma((n, CHUNKS)),
            dma((n,)),
            dma((n,)),
            dma((n,)),
            dma((n,)),
        ],
        compiler_params=pltpu.CompilerParams(
            collective_id=0, has_side_effects=True, vmem_limit_bytes=44 * 2**20
        ),
    )(*arrays)
    return pl.pallas_call(
        hand_out,
        out_shape=out_shape,
        in_specs=[vmem, vmem, vmem],
        out_specs=(hbm, hbm, hbm),
        scratch_shapes=[dma((3,))],
        compiler_params=pltpu.CompilerParams(vmem_limit_bytes=4 * 2**20),
    )(*results)


def solution(mesh):
    spec = P(("doc", "seq"), None)
    return jax.shard_map(
        functools.partial(body, mesh.shape["seq"]),
        mesh=mesh,
        in_specs=(spec, spec, spec, P(("doc", "seq"))),
        out_specs=(spec, spec, spec),
        check_vma=False,
    )
```

time: 32.7 us -> 22.9 us (0.70)
  Pallas kernels: 28.6 us -> 22.1 us
  local copies, waits for them, and re-layouts: 3.21 us -> 0 us
    pallas_call x1 -> x2, Pallas kernels: 28.6 us -> 22.1 us  [the longest x1 21.3 us: body(): pl.pallas_call(functools.partial(kernel, n), out_shape=out_shape, in_spec...]
    unnamed x7 -> x0, local copies, waits for them, and re-layouts: 3.21 us -> none
where the time goes in v2:
time: 22.9 us; the launch traced here: 22.7 us
  Pallas kernels  22.1 us (97%)
  between operations  0.64 us (3%)
    pallas_call x1, Pallas kernels, body(): pl.pallas_call(functools.partial(kernel, n), out_shape=out_shape, in_spec...  21.3 us
    pallas_call x1, Pallas kernels, body(): pl.pallas_call(hand_out, out_shape=out_shape, in_specs=[vmem, vmem, vmem]...  0.83 us

profile of v2, /device:TPU:0, one launch (start us, length us, event | category | flops | bytes accessed | tf_op | source)
XLA Modules:
  0.0 22.7 jit_solution(14276432225407626862)
XLA Ops:
  0.6 21.3 %shard_map.67 = (bf16[512,512]{1,0:T(8,128)(2,1)S(1)}, f32[32,128]{1,0:T(8,128)S(1)}, f32[32,128]{1,0:T(8,128)S(1)}) custom-call(s32[32]{0:T(128)} %starts_hbm.1, bf16[512,512]{1,0:T(8,128)(2,1)} %q_hbm.1, bf16[512,128]{1,0:T(8,128)(2,1)} %k_hbm.1, bf16[512,128]{1,0:T(8,128)(2,1)} %v_hbm.1), custom_call_target="tpu_custom_call" | custom-call | tf_op jit(solution)/shard_map/pallas_call | solution.py:333
  21.9 0.8 %shard_map.68 = (bf16[512,512]{1,0:T(8,128)(2,1)}, f32[32,128]{1,0:T(8,128)}, f32[32,128]{1,0:T(8,128)}) custom-call(bf16[512,512]{1,0:T(8,128)(2,1)S(1)} %get-tuple-element.6.gap, f32[32,128]{1,0:T(8,128)S(1)} %get-tuple-element.7.gk, f32[32,128]{1,0:T(8,128)S(1)} %get-tuple-element.8.gv), custom_call_target="tpu_custom_call" | custom-call | tf_op jit(solution)/shard_map/pallas_call | solution.py:362

commit v3 on v2

--- a/solution.py
+++ b/solution.py
@@ -49,6 +49,8 @@
     beac,
     state_m,
     state_acc,
+    own_m,
+    own_acc,
     student,
     probs,
     stage,
@@ -140,8 +142,7 @@
 
         @pl.when(c > chip)
         def _():
-            for i in range(CHUNKS):
-                direct(c, i).start()
+            direct(c, 0).start()
 
     @pl.when(core == 0)
     def _():
@@ -166,6 +167,13 @@
             beacon_copy(s).start()
             beac[s] = jnp.zeros((count, 2 * dim), jnp.bfloat16)
 
+    for c in range(1, chips):
+
+        @pl.when(c > chip)
+        def _():
+            for i in range(1, CHUNKS):
+                direct(c, i).start()
+
     loads[2].wait()
 
     for h in range(heads):
@@ -178,28 +186,11 @@
             s = jnp.where(lax.broadcasted_iota(jnp.int32, (half, keys), 1) <= row_pos, s, NEG)
             m = jnp.broadcast_to(jnp.max(s, axis=1, keepdims=True), (half, dim))
             p = jnp.exp2((s - wide(m, keys)) * fold).astype(jnp.bfloat16)
+            acc = dot_nn(p, with_ones(kv[me, :keys, dim:]))
             state_m[h, rows] = m
-            state_acc[h, rows] = dot_nn(p, with_ones(kv[me, :keys, dim:]))
-
-    for s in range(n - 1):
-
-        @pl.when(s < me)
-        def _():
-            beacon_arrival(s).wait_recv()
-
-    beacons = beac[...].reshape(nb, 2 * dim)
-    for h in range(heads):
-        cols = pl.ds(h * dim, dim)
-        s = dot_nt(q_ref[:, cols], beacons[:, :dim])
-        s = jnp.where(lax.broadcasted_iota(jnp.int32, (tok, nb), 1) < me * count, s, NEG)
-        m_own = state_m[h]
-        m = jnp.maximum(m_own, jnp.broadcast_to(jnp.max(s, axis=1, keepdims=True), (tok, dim)))
-        w = jnp.exp2((s - wide(m, nb)) * fold)
-        acc = state_acc[h] * wide(jnp.exp2((m_own - m) * fold), 2 * dim)
-        acc = acc + dot_nn(w.astype(jnp.bfloat16), with_ones(beacons[:, dim:]))
-        inverse = 1.0 / acc[:, dim:]
-        student[h] = acc[:, :dim] * inverse
-        probs[h] = (w * wide(inverse, nb)).astype(jnp.bfloat16)
+            state_acc[h, rows] = acc
+            own_m[h, rows] = m
+            own_acc[h, rows] = acc
 
     def fold_block(slot, first, keys):
         for h in range(heads):
@@ -223,23 +214,54 @@
             arrival(me - 1, i).wait_recv()
         fold_block(me - 1, 0, tok)
 
-    def direct_block(c, carry):
+    def direct_piece(c, i):
+        arrival(2 * c + core, i).wait_recv()
+        forward(c, i).start()
+        fold_block(2 * c + core, i * piece, piece)
+
+    def passed_piece(c, i):
+        arrival(2 * c + 1 - core, i).wait_recv()
+        fold_block(2 * c + 1 - core, i * piece, piece)
+
+    @pl.when(chip > 0)
+    def _():
+        direct_piece(0, 0)
+
+    for s in range(n - 1):
+
+        @pl.when(s < me)
+        def _():
+            beacon_arrival(s).wait_recv()
+
+    beacons = beac[...].reshape(nb, 2 * dim)
+    for h in range(heads):
+        cols = pl.ds(h * dim, dim)
+        s = dot_nt(q_ref[:, cols], beacons[:, :dim])
+        s = jnp.where(lax.broadcasted_iota(jnp.int32, (tok, nb), 1) < me * count, s, NEG)
+        m_own = own_m[h]
+        m = jnp.maximum(m_own, jnp.broadcast_to(jnp.max(s, axis=1, keepdims=True), (tok, dim)))
+        w = jnp.exp2((s - wide(m, nb)) * fold)
+        acc = own_acc[h] * wide(jnp.exp2((m_own - m) * fold), 2 * dim)
+        acc = acc + dot_nn(w.astype(jnp.bfloat16), with_ones(beacons[:, dim:]))
+        inverse = 1.0 / acc[:, dim:]
+        student[h] = acc[:, :dim] * inverse
+        probs[h] = (w * wide(inverse, nb)).astype(jnp.bfloat16)
+
+    @pl.when(chip > 0)
+    def _():
+        passed_piece(0, 0)
+        for i in range(1, CHUNKS):
+            direct_piece(0, i)
+            passed_piece(0, i)
+
+    def earlier_chip(c, carry):
         for i in range(CHUNKS):
-            arrival(2 * c + core, i).wait_recv()
-            forward(c, i).start()
-            fold_block(2 * c + core, i * piece, piece)
+            direct_piece(c, i)
+            passed_piece(c, i)
         return carry
 
-    lax.fori_loop(0, chip, direct_block, 0)
-
-    def passed_block(c, carry):
-        slot = 2 * c + 1 - core
-        for i in range(CHUNKS):
-            arrival(slot, i).wait_recv()
-        fold_block(slot, 0, tok)
-        return carry
-
-    lax.fori_loop(0, chip, passed_block, 0)
+    if chips > 2:
+        lax.fori_loop(1, chip, earlier_chip, 0)
 
     values = beac[...].reshape(nb, 2 * dim)[:, dim:]
     sum_k = jnp.zeros((nb, dim), jnp.float32)
@@ -343,6 +365,8 @@
             pltpu.VMEM((heads, tok, dim), jnp.float32),
             pltpu.VMEM((heads, tok, 2 * dim), jnp.float32),
             pltpu.VMEM((heads, tok, dim), jnp.float32),
+            pltpu.VMEM((heads, tok, 2 * dim), jnp.float32),
+            pltpu.VMEM((heads, tok, dim), jnp.float32),
             pltpu.VMEM((heads, tok, n * count), jnp.bfloat16),
             pltpu.VMEM((n, count, 2 * dim), jnp.bfloat16),
             pltpu.VMEM((n, count, 2 * dim), jnp.bfloat16),

time: 22.9 us -> 19 us (0.83)
  Pallas kernels: 22.1 us -> 18.3 us
    pallas_call x1, Pallas kernels: 21.3 us -> 17.4 us  [body(): pl.pallas_call(functools.partial(kernel, n), out_shape=out_shape, in_spec...]
where the time goes in v3:
time: 19 us; the launch traced here: 18.9 us
  Pallas kernels  18.3 us (96%)
  between operations  0.64 us (3%)
    pallas_call x1, Pallas kernels, body(): pl.pallas_call(functools.partial(kernel, n), out_shape=out_shape, in_spec...  17.4 us
    pallas_call x1, Pallas kernels, body(): pl.pallas_call(hand_out, out_shape=out_shape, in_specs=[vmem, vmem, vmem]...  0.83 us

profile of v3, /device:TPU:0, one launch (start us, length us, event | category | flops | bytes accessed | tf_op | source)
XLA Modules:
  0.0 18.9 jit_solution(17499730074755642597)
XLA Ops:
  0.6 17.4 %shard_map.67 = (bf16[512,512]{1,0:T(8,128)(2,1)S(1)}, f32[32,128]{1,0:T(8,128)S(1)}, f32[32,128]{1,0:T(8,128)S(1)}) custom-call(s32[32]{0:T(128)} %starts_hbm.1, bf16[512,512]{1,0:T(8,128)(2,1)} %q_hbm.1, bf16[512,128]{1,0:T(8,128)(2,1)} %k_hbm.1, bf16[512,128]{1,0:T(8,128)(2,1)} %v_hbm.1), custom_call_target="tpu_custom_call" | custom-call | tf_op jit(solution)/shard_map/pallas_call | solution.py:355
  18.1 0.8 %shard_map.68 = (bf16[512,512]{1,0:T(8,128)(2,1)}, f32[32,128]{1,0:T(8,128)}, f32[32,128]{1,0:T(8,128)}) custom-call(bf16[512,512]{1,0:T(8,128)(2,1)S(1)} %get-tuple-element.6.gap, f32[32,128]{1,0:T(8,128)S(1)} %get-tuple-element.7.gk, f32[32,128]{1,0:T(8,128)S(1)} %get-tuple-element.8.gv), custom_call_target="tpu_custom_call" | custom-call | tf_op jit(solution)/shard_map/pallas_call | solution.py:386
